TPU v7x, 32 devices: a whole 2x2x4 slice. The times are simulated.
32 devices in a mesh: kx: 8 (over z, x), cz: 4 (over y, core).
Axes of the slice: x: 2, y: 2, z: 4, core: 2. Of those that a mesh axis runs over, the one named last changes fastest.
Arguments:
- field_modes: bfloat16 [512, 4, 12288], P('cz', None, 'kx'), may hold values from -6 to 6
- cotangent: bfloat16 [512, 4, 12288], P('cz', None, 'kx'), may hold values from -6 to 6
Outputs:
- mode_gradient: bfloat16 [512, 4, 12288], P('cz', None, 'kx')
All inputs are finite; a program needn't handle non-finite values.
Results may differ from a plain program's by a relative error of at most 0.009.
Values may be sent and summed in bfloat16 or wider, within the bound.
A program may use at most 128 MiB of HBM per device.

v0:
```python
import functools
import math

import jax
import jax.numpy as jnp
import numpy as np
from jax import lax
from jax.experimental import pallas as pl
from jax.experimental.pallas import tpu as pltpu
from jax.sharding import PartitionSpec as P

MZ = 768
Y = 16
MESH = pl.DeviceIdType.MESH


def cosine_table(rows, columns):
    position = (np.arange(columns)[None, :] * (2 * np.arange(rows)[:, None] + 1)) % (4 * rows)
    return np.cos(np.pi * position / (2 * rows)).astype(np.float32)


def hartley_table(points):
    index = np.arange(points)
    phases = 2.0 * np.pi * ((index[:, None] * index[None, :]) % points) / points
    return (np.cos(phases) + np.sin(phases)) / math.sqrt(points)


def matmul(a, b):
    return jnp.dot(a, b, preferred_element_type=jnp.float32)


def kernel(
    nkx, ncz, shares,
    field_modes, cotangent, hartley_in, lift_fields_in, lift_adjoint_in, lower_in,
    out,
    raw, hartley, lift_fields, lift_adjoint, lower, raw_sem, table_sem,
    wide, rows, held, mixed, halves, points, total, flux, lowered, turned, result,
    in_send, in_recv, swap_send, swap_recv, back_send, back_recv, out_send, out_recv,
):
    local_k, fields, columns = field_modes.shape
    rows_y = rows.shape[1]
    local_m = columns // rows_y
    per_share = ncz // shares
    points_x = hartley.shape[0]
    points_z = lift_fields.shape[2]
    share_x = points_x // shares
    i, j = lax.axis_index("kx"), lax.axis_index("cz")
    linear = i * ncz + j
    my_y, my_share = linear // shares, lax.rem(linear, shares)
    to_share = j // per_share
    my_part = lax.rem(j, per_share)
    my_slot = i * per_share + my_part
    stays = to_share == my_share
    far = rows_y // 2
    order = ((0, 2), (1, 0), (1, 1), (1, 3), (0, 0), (0, 1), (0, 3), (1, 2))
    def device(target):
        return {"kx": target // ncz, "cz": lax.rem(target, ncz)}

    raw_copies = [
        pltpu.make_async_copy(array, raw.at[a], raw_sem.at[a]) for a, array in enumerate((field_modes, cotangent))
    ]
    table_copies = [
        pltpu.make_async_copy(source, target, table_sem.at[n])
        for n, (source, target) in enumerate(
            (
                (hartley_in, hartley),
                (lift_fields_in, lift_fields),
                (lift_adjoint_in, lift_adjoint),
                (lower_in, lower),
            )
        )
    ]
    for copy in raw_copies + table_copies:
        copy.start()
    barrier = pltpu.get_barrier_semaphore()

    def greet(step, carry):
        pl.semaphore_signal(
            barrier, inc=1, device_id=device(lax.rem(linear + step, nkx * ncz)), device_id_type=MESH
        )
        return carry

    lax.fori_loop(1, nkx * ncz, greet, 0)
    tables = (lift_fields, lift_adjoint)

    def block(ref, slot):
        part = lax.rem(slot, per_share)
        rows = pl.ds(pl.multiple_of((slot // per_share) * local_m, local_m), local_m)
        columns = pl.ds(pl.multiple_of(part * local_k, local_k), local_k) if per_share > 1 else slice(None)
        return ref.at[rows, columns]

    def other(mine, step):
        half = jnp.where(step < far, 1 - mine // far, mine // far)
        return half * far + lax.rem(mine + 1 + step, far)

    def wait(ref, sem):
        pltpu.make_async_copy(ref, ref, sem).wait()

    def in_remote(h, y):
        return pltpu.make_async_remote_copy(
            src_ref=rows.at[h, y],
            dst_ref=block(held.at[h], my_slot),
            send_sem=in_send,
            recv_sem=in_recv.at[h],
            device_id=device(y * shares + to_share),
            device_id_type=MESH,
        )

    chunk = 128 if columns % 128 == 0 else columns

    for h, (a, f) in enumerate(order):
        if h < 2:
            raw_copies[h].wait()

        def turn(step, carry):
            here = pl.ds(pl.multiple_of(step * chunk, chunk), chunk)
            wide[here, :] = raw[a, :, f, here].astype(jnp.float32).T
            return carry

        lax.fori_loop(0, columns // chunk, turn, 0)
        for y in range(rows_y):
            rows[h, y] = wide[pl.ds(y, local_m, stride=rows_y), :].astype(jnp.bfloat16)
        if h == 0:
            pl.semaphore_wait(barrier, nkx * ncz - 1)

        def send(step, carry):
            in_remote(h, other(my_y, step)).start()
            return carry

        lax.fori_loop(0, rows_y - 1, send, 0)

        @pl.when(stays)
        def _():
            pltpu.make_async_copy(rows.at[h, my_y], block(held.at[h], my_slot), in_recv.at[h]).start()

        @pl.when(jnp.logical_not(stays))
        def _():
            in_remote(h, my_y).start()

    def share_rows(q):
        return pl.ds(pl.multiple_of(q * share_x, share_x), share_x)

    def mix(h):
        wait(held.at[h], in_recv.at[h])
        mixed[h] = matmul(hartley[...], held[h]).astype(jnp.bfloat16)
        for step in range(1, shares):
            q = lax.rem(my_share + step, shares)
            pltpu.make_async_remote_copy(
                src_ref=mixed.at[h, share_rows(q), :],
                dst_ref=halves.at[h, my_share],
                send_sem=swap_send,
                recv_sem=swap_recv.at[h],
                device_id=device(my_y * shares + q),
                device_id_type=MESH,
            ).start()
        pltpu.make_async_copy(
            mixed.at[h, share_rows(my_share), :], halves.at[h, my_share], swap_recv.at[h]
        ).start()

    block_z = 256 if points_z % 256 == 0 else points_z

    def lift(h, use):
        wait(halves.at[h], swap_recv.at[h])
        table = tables[order[h][0]]

        def one(step, carry):
            here = pl.ds(pl.multiple_of(step * block_z, block_z), block_z)
            value = matmul(halves[h, 0], table[0, :, here])
            for q in range(1, shares):
                value += matmul(halves[h, q], table[q, :, here])
            use(here, value)
            return carry

        lax.fori_loop(0, points_z // block_z, one, 0)

    def leave(f):
        for q in range(shares):
            lowered[f, q] = matmul(flux[...], lower[q]).astype(jnp.bfloat16)
        for step in range(1, shares):
            q = lax.rem(my_share + step, shares)
            pltpu.make_async_remote_copy(
                src_ref=lowered.at[f, q],
                dst_ref=turned.at[f, share_rows(my_share), :],
                send_sem=back_send,
                recv_sem=back_recv.at[f],
                device_id=device(my_y * shares + q),
                device_id_type=MESH,
            ).start()
        pltpu.make_async_copy(
            lowered.at[f, my_share], turned.at[f, share_rows(my_share), :], back_recv.at[f]
        ).start()

    def out_remote(f, slot):
        target = (slot // per_share) * ncz + my_share * per_share + lax.rem(slot, per_share)
        return pltpu.make_async_remote_copy(
            src_ref=block(result.at[f], slot),
            dst_ref=out.at[my_y, f],
            send_sem=out_send,
            recv_sem=out_recv.at[f],
            device_id=device(target),
            device_id_type=MESH,
        )

    def finish(f):
        wait(turned.at[f], back_recv.at[f])
        result[f] = matmul(hartley[...], turned[f]).astype(jnp.bfloat16)

        def send(step, carry):
            out_remote(f, other(my_slot, step)).start()
            return carry

        lax.fori_loop(0, rows_y - 1, send, 0)

        @pl.when(stays)
        def _():
            pltpu.make_async_copy(block(result.at[f], my_slot), out.at[my_y, f], out_recv.at[f]).start()

        @pl.when(jnp.logical_not(stays))
        def _():
            out_remote(f, my_slot).start()

    def keep(h):
        def use(here, value):
            points[h, :, here] = value
        return use

    def keep_and_flux(h):
        def use(here, value):
            points[h, :, here] = value
            flux[:, here] = (value * points[0, :, here]).astype(jnp.bfloat16)
        return use

    def first(here, value):
        total[:, here] = points[1, :, here] * value

    def add(h):
        def use(here, value):
            total[:, here] += points[h, :, here] * value
        return use

    def last(here, value):
        flux[:, here] = (total[:, here] + 2.0 * value * points[0, :, here]).astype(jnp.bfloat16)

    for copy in table_copies:
        copy.wait()
    mix(0)
    mix(1)
    lift(0, keep(0))
    lift(1, keep_and_flux(1))
    leave(0)
    mix(2)
    finish(0)
    lift(2, keep_and_flux(2))
    leave(1)
    mix(3)
    finish(1)
    lift(3, keep_and_flux(3))
    leave(3)
    mix(4)
    finish(3)
    lift(4, first)
    mix(5)
    lift(5, add(2))
    mix(6)
    lift(6, add(3))
    mix(7)
    lift(7, last)
    leave(2)
    finish(2)

    @pl.when(stays)
    def _():
        wait(rows.at[:, pl.ds(0, rows_y - 1)], in_send)

    @pl.when(jnp.logical_not(stays))
    def _():
        wait(rows, in_send)

    if shares > 1:
        wait(mixed.at[:, pl.ds(0, share_x * (shares - 1)), :], swap_send)
        wait(lowered.at[:, pl.ds(0, shares - 1)], back_send)

    @pl.when(stays)
    def _():
        wait(out.at[pl.ds(0, rows_y - 1)], out_send)

    @pl.when(jnp.logical_not(stays))
    def _():
        wait(out, out_send)

    for f in range(fields):
        wait(out.at[:, f], out_recv.at[f])


def on_device(nkx, ncz, field_modes, cotangent):
    local_k, fields, columns = field_modes.shape
    local_m = columns // Y
    modes_z, points_x = local_k * ncz, local_m * nkx
    shares = nkx * ncz // Y
    group_k = modes_z // shares
    share_x = points_x // shares
    bf16 = jnp.bfloat16

    cosines = cosine_table(MZ, modes_z)
    synthesis = jnp.asarray((cosines * math.sqrt(2.0 / modes_z)).astype(bf16))
    projection = jnp.asarray((cosines * math.sqrt(2.0 / MZ)).astype(bf16))
    hartley = jnp.asarray(hartley_table(points_x).astype(np.float32).astype(bf16))
    lift_fields = synthesis.T.reshape(shares, group_k, MZ)
    lift_adjoint = projection.T.reshape(shares, group_k, MZ)
    lower = synthesis.reshape(MZ, shares, group_k).transpose(1, 0, 2)

    hbm = pl.BlockSpec(memory_space=pltpu.HBM)
    dma = pltpu.SemaphoreType.DMA
    out = pl.pallas_call(
        functools.partial(kernel, nkx, ncz, shares),
        out_shape=jax.ShapeDtypeStruct((Y, fields, local_m, local_k), bf16),
        in_specs=[hbm] * 6,
        out_specs=pl.BlockSpec(memory_space=pl.ANY),
        scratch_shapes=[
            pltpu.VMEM((2, local_k, fields, columns), bf16),
            pltpu.VMEM(hartley.shape, bf16),
            pltpu.VMEM(lift_fields.shape, bf16),
            pltpu.VMEM(lift_adjoint.shape, bf16),
            pltpu.VMEM(lower.shape, bf16),
            dma((2,)), dma((4,)),
            pltpu.VMEM((columns, local_k), jnp.float32),
            pltpu.VMEM((2 * fields, Y, local_m, local_k), bf16),
            pltpu.VMEM((2 * fields, points_x, group_k), bf16),
            pltpu.VMEM((2 * fields, points_x, group_k), bf16),
            pltpu.VMEM((2 * fields, shares, share_x, group_k), bf16),
            pltpu.VMEM((fields, share_x, MZ), jnp.float32),
            pltpu.VMEM((share_x, MZ), jnp.float32),
            pltpu.VMEM((share_x, MZ), bf16),
            pltpu.VMEM((fields, shares, share_x, group_k), bf16),
            pltpu.VMEM((fields, points_x, group_k), bf16),
            pltpu.VMEM((fields, points_x, group_k), bf16),
            dma, dma((2 * fields,)), dma, dma((2 * fields,)),
            dma, dma((fields,)), dma, dma((fields,)),
        ],
        compiler_params=pltpu.CompilerParams(has_side_effects=True, vmem_limit_bytes=63 * 2**20, collective_id=0),
    )(field_modes, cotangent, hartley, lift_fields, lift_adjoint, lower)
    return out.transpose(3, 1, 2, 0).reshape(local_k, fields, columns)


def solution(mesh):
    return jax.shard_map(
        functools.partial(on_device, mesh.shape["kx"], mesh.shape["cz"]),
        mesh=mesh,
        in_specs=(P("cz", None, "kx"), P("cz", None, "kx")),
        out_specs=P("cz", None, "kx"),
        check_vma=False,
    )
```

profile of v0, /device:TPU:0, one launch (start us, length us, event | category | flops | bytes accessed | tf_op | source)
XLA Modules:
  0.0 116.3 jit_solution(1519929906296791100)
XLA Ops:
  0.0 111.4 %shard_map.55 = bf16[16,4,96,128]{3,2,1,0:T(8,128)(2,1)} custom-call(bf16[128,4,1536]{2,1,0:T(4,128)(2,1)} %field_modes.1, bf16[128,4,1536]{2,1,0:T(4,128)(2,1)} %cotangent.1, bf16[768,768]{1,0:T(8,128)(2,1)} %constant.8.clone.hartley_in, bf16[2,256,768]{2,1,0:T(8,128)(2,1)} %constant.10.lift_fields_in, bf16[2,256,768]{2,1,0:T(8,128)(2,1)} %constant.12.lift_adjoint_in, ...), custom_call_target="tpu_custom_call" | custom-call | tf_op jit(solution)/shard_map/pallas_call | solution.py:314
  111.5 2.4 %copy.6 = bf16[128,4,96,16]{0,3,2,1:T(8,128)(2,1)S(1)} copy(bf16[128,4,96,16]{0,2,1,3:T(8,128)(2,1)} %bitcast.3) | data formatting | bytes 3145728 | tf_op jit(solution)/shard_map/transpose | solution.py:342
  113.9 2.5 %copy.7 = bf16[128,4,1536]{2,1,0:T(4,128)(2,1)} copy(bf16[128,4,1536]{0,2,1:T(8,128)(2,1)S(1)} %bitcast.2) | data formatting | bytes 3145728 | tf_op jit(solution)/shard_map/reshape | solution.py:342
where the time goes:
time: 116 us
  Pallas kernels  111 us (96%)
  local copies, waits for them, and re-layouts  4.89 us (4%)
    pallas_call x1, Pallas kernels, on_device(): pl.pallas_call(functools.partial(kernel, nkx, ncz, shares), out_shape=jax...  111 us
    reshape x1, local copies, waits for them, and re-layouts, on_device(): return out.transpose(3, 1, 2, 0).reshape(local_k, fields, columns)  2.46 us
    transpose x1, local copies, waits for them, and re-layouts, on_device(): return out.transpose(3, 1, 2, 0).reshape(local_k, fields, columns)  2.42 us

commit v1 on v0

v1 whole, which is shorter than its diff:
```python
import functools
import math

import jax
import jax.numpy as jnp
import numpy as np
from jax import lax
from jax.experimental import pallas as pl
from jax.experimental.pallas import tpu as pltpu
from jax.sharding import PartitionSpec as P

MZ = 768
Y = 16
MESH = pl.DeviceIdType.MESH


def cosine_table(rows, columns):
    position = (np.arange(columns)[None, :] * (2 * np.arange(rows)[:, None] + 1)) % (4 * rows)
    return np.cos(np.pi * position / (2 * rows)).astype(np.float32)


def hartley_table(points):
    index = np.arange(points)
    phases = 2.0 * np.pi * ((index[:, None] * index[None, :]) % points) / points
    return (np.cos(phases) + np.sin(phases)) / math.sqrt(points)


def matmul(a, b):
    return jnp.dot(a, b, preferred_element_type=jnp.float32)


def matmul_t(a, b):
    return lax.dot_general(a, b, (((1,), (1,)), ((), ())), preferred_element_type=jnp.float32)


def kernel(
    nkx, ncz, pieces,
    field_modes, cotangent, tables_in,
    out,
    raw, tables, raw_sem, table_sem, ready,
    wide, rows, held, mixed, parts, points, total, flux, lowered, turned, result, landed,
    in_send, in_recv, swap_send, swap_recv, back_send, back_recv, out_send, out_recv,
):
    local_k, fields, columns = field_modes.shape
    rows_y = rows.shape[1]
    local_m = columns // rows_y
    own_rows = rows_y // nkx
    points_x = local_m * nkx
    points_z = points.shape[2]
    modes_z = local_k * ncz
    share_x = points_x // ncz
    aligned = local_k % 128 == 0
    i, j = lax.axis_index("kx"), lax.axis_index("cz")
    order = ((0, 2), (1, 0), (1, 1), (1, 3), (0, 0), (0, 1), (0, 3), (1, 2))

    places = nkx // 2
    place, column = i // 2, lax.rem(i, 2)
    above, below = place + 1 < places, place > 0
    near = 1 + jnp.where(above, 1, 0) + jnp.where(below, 1, 0)

    def at(row_owner, mode_owner):
        return {"kx": row_owner, "cz": mode_owner}

    def wait(ref, sem):
        pltpu.make_async_copy(ref, ref, sem).wait()

    piece = columns // pieces
    raw_copies = [
        [
            pltpu.make_async_copy(
                array.at[:, :, pl.ds(p * piece, piece)], raw.at[a, :, :, pl.ds(p * piece, piece)], raw_sem.at[a, p]
            )
            for p in range(pieces)
        ]
        for a, array in enumerate((field_modes, cotangent))
    ]
    table_copy = pltpu.make_async_copy(tables_in, tables, table_sem)
    for copy in raw_copies[0]:
        copy.start()
    barrier = pltpu.get_barrier_semaphore()

    def signal_near(sem):
        pl.semaphore_signal(sem, inc=1, device_id=at(place * 2 + 1 - column, j), device_id_type=MESH)

        @pl.when(above)
        def _():
            pl.semaphore_signal(sem, inc=1, device_id=at(i + 2, j), device_id_type=MESH)

        @pl.when(below)
        def _():
            pl.semaphore_signal(sem, inc=1, device_id=at(i - 2, j), device_id_type=MESH)

    signal_near(barrier)
    for step in range(1, ncz):
        pl.semaphore_signal(barrier, inc=1, device_id=at(i, lax.rem(j + step, ncz)), device_id_type=MESH)
    for copy in raw_copies[1]:
        copy.start()

    hartley = tables.at[pl.ds(0, points_x)]
    lifts = [tables.at[pl.ds(points_x + n * modes_z, modes_z)] for n in range(2)]
    chunk = 128 if piece % 128 == 0 else piece

    def prepare(h):
        a, f = order[h]

        def turn(step, carry):
            here = pl.ds(pl.multiple_of(step * chunk, chunk), chunk)
            wide[here, :] = raw[a, :, f, here].astype(jnp.float32).T
            return carry

        for p in range(pieces):
            if h < 2:
                raw_copies[a][p].wait()
                lax.fori_loop(p * (piece // chunk), (p + 1) * (piece // chunk), turn, 0)
        if h >= 2:
            lax.fori_loop(0, columns // chunk, turn, 0)
        for y in range(rows_y):
            rows[h, y] = wide[pl.ds(y, local_m, stride=rows_y), :].astype(jnp.bfloat16)

    def in_place(h):
        return held.at[h, :, pl.ds(pl.multiple_of(i * local_m, local_m), local_m)]

    def send_in(h, target):
        pltpu.make_async_remote_copy(
            src_ref=rows.at[h, pl.ds(target * own_rows, own_rows)],
            dst_ref=in_place(h),
            send_sem=in_send,
            recv_sem=in_recv.at[h],
            device_id=at(target, j),
            device_id_type=MESH,
        ).start()

    def keep_in(h):
        pltpu.make_async_copy(rows.at[h, pl.ds(i * own_rows, own_rows)], in_place(h), in_recv.at[h]).start()

    def flip(index, step):
        bit = 1
        target = index
        while bit < nkx:
            if step & bit:
                target = target + bit * (1 - 2 * lax.rem(index // bit, 2))
            bit *= 2
        return target

    half = nkx // 2
    steps = [s for s in range(1, half)] + [s for s in range(half, nkx) if s % 2] + [s for s in range(half, nkx) if not s % 2]

    def others():
        if nkx & (nkx - 1):
            return [lax.rem(i + s, nkx) for s in range(1, nkx)]
        return [flip(i, s) for s in steps]

    def send_at_distance(h, distance):
        for hops, side in ((distance, 0), (distance - 1, 1)):
            facing = place * 2 + (column if side == 0 else 1 - column)
            if hops == 0:
                send_in(h, facing)
            elif hops < places:
                @pl.when(place + hops < places)
                def _():
                    send_in(h, facing + 2 * hops)

                @pl.when(place >= hops)
                def _():
                    send_in(h, facing - 2 * hops)

    prepare(0)
    pl.semaphore_wait(barrier, near + ncz - 1)
    send_at_distance(0, 1)
    for distance in range(2, places + 1):
        sem = ready.at[distance - 2]
        signal_near(sem)
        pl.semaphore_wait(sem, near)
        send_at_distance(0, distance)
    keep_in(0)
    table_copy.start()
    for h in range(1, 2 * fields):
        prepare(h)
        for target in others():
            send_in(h, target)
        keep_in(h)

    def share_rows(q):
        return pl.ds(pl.multiple_of(q * share_x, share_x), share_x)

    def lanes(r):
        return slice(r * local_k, (r + 1) * local_k)

    def transform(target, source):
        if aligned:
            joined = source[0] if len(source) == 1 else jnp.concatenate(source, axis=1)
            value = matmul(hartley[...], joined).astype(jnp.bfloat16)
            for r in range(own_rows):
                target(r, value[:, lanes(r)])
        else:
            for r in range(own_rows):
                target(r, matmul(hartley[...], source[r]).astype(jnp.bfloat16))

    def mix(h):
        wait(held.at[h], in_recv.at[h])

        def keep(r, value):
            mixed[h, :, lanes(r)] = value

        transform(keep, [held[h, r] for r in range(own_rows)])
        for step in range(1, ncz):
            q = lax.rem(j + step, ncz)
            pltpu.make_async_remote_copy(
                src_ref=mixed.at[h, share_rows(q), :],
                dst_ref=parts.at[h, j],
                send_sem=swap_send,
                recv_sem=swap_recv.at[h],
                device_id=at(i, q),
                device_id_type=MESH,
            ).start()
        pltpu.make_async_copy(mixed.at[h, share_rows(j), :], parts.at[h, j], swap_recv.at[h]).start()

    block_z = 256 if points_z % 256 == 0 else points_z

    def lift(h, use):
        wait(parts.at[h], swap_recv.at[h])
        table = lifts[order[h][0]]

        def one(step, carry):
            here = pl.ds(pl.multiple_of(step * block_z, block_z), block_z)
            if aligned:
                joined = jnp.concatenate(
                    [
                        jnp.concatenate([parts[h, q, :, lanes(r)] for q in range(ncz)], axis=1)
                        for r in range(own_rows)
                    ],
                    axis=0,
                )
                use(slice(None), here, matmul(joined, table[:, here]))
            else:
                for r in range(own_rows):
                    value = matmul(parts[h, 0, :, lanes(r)], table[0:local_k, here])
                    for q in range(1, ncz):
                        value += matmul(parts[h, q, :, lanes(r)], table[q * local_k:(q + 1) * local_k, here])
                    use(slice(r * share_x, (r + 1) * share_x), here, value)
            return carry

        lax.fori_loop(0, points_z // block_z, one, 0)

    def leave(f):
        if aligned:
            value = matmul_t(flux[...], lifts[0][...]).astype(jnp.bfloat16)
            for q in range(ncz):
                for r in range(own_rows):
                    lowered[f, q, :, lanes(r)] = value[r * share_x:(r + 1) * share_x, lanes(q)]
        else:
            for q in range(ncz):
                for r in range(own_rows):
                    lowered[f, q, :, lanes(r)] = matmul_t(
                        flux[r * share_x:(r + 1) * share_x, :], lifts[0][q * local_k:(q + 1) * local_k, :]
                    ).astype(jnp.bfloat16)
        for step in range(1, ncz):
            q = lax.rem(j + step, ncz)
            pltpu.make_async_remote_copy(
                src_ref=lowered.at[f, q],
                dst_ref=turned.at[f, share_rows(j), :],
                send_sem=back_send,
                recv_sem=back_recv.at[f],
                device_id=at(i, q),
                device_id_type=MESH,
            ).start()
        pltpu.make_async_copy(lowered.at[f, j], turned.at[f, share_rows(j), :], back_recv.at[f]).start()

    def out_block(f, target):
        return result.at[f, :, pl.ds(pl.multiple_of(target * local_m, local_m), local_m)]

    def out_place(f):
        return landed.at[f, pl.ds(i * own_rows, own_rows)]

    def finish(f):
        wait(turned.at[f], back_recv.at[f])

        def keep(r, value):
            result[f, r] = value

        transform(keep, [turned[f, :, lanes(r)] for r in range(own_rows)])
        for target in others():
            pltpu.make_async_remote_copy(
                src_ref=out_block(f, target),
                dst_ref=out_place(f),
                send_sem=out_send,
                recv_sem=out_recv.at[f],
                device_id=at(target, j),
                device_id_type=MESH,
            ).start()
        pltpu.make_async_copy(out_block(f, i), out_place(f), out_recv.at[f]).start()

    def keep(h):
        def use(part, here, value):
            points[h, part, here] = value
        return use

    def keep_and_flux(h):
        def use(part, here, value):
            points[h, part, here] = value
            flux[part, here] = (value * points[0, part, here]).astype(jnp.bfloat16)
        return use

    def first(part, here, value):
        total[part, here] = points[1, part, here] * value

    def add(h):
        def use(part, here, value):
            total[part, here] += points[h, part, here] * value
        return use

    def last(part, here, value):
        flux[part, here] = (total[part, here] + 2.0 * value * points[0, part, here]).astype(jnp.bfloat16)

    table_copy.wait()
    mix(0)
    mix(1)
    lift(0, keep(0))
    lift(1, keep_and_flux(1))
    leave(0)
    mix(2)
    finish(0)
    lift(2, keep_and_flux(2))
    leave(1)
    mix(3)
    finish(1)
    lift(3, keep_and_flux(3))
    leave(3)
    mix(4)
    finish(3)
    lift(4, first)
    mix(5)
    lift(5, add(2))
    mix(6)
    lift(6, add(3))
    mix(7)
    lift(7, last)
    leave(2)
    finish(2)

    for f in (0, 1, 3, 2):
        wait(landed.at[f], out_recv.at[f])
        for y in range(rows_y):
            wide[pl.ds(y, local_m, stride=rows_y), :] = landed[f, y].astype(jnp.float32)

        def settle(step, carry):
            here = pl.ds(pl.multiple_of(step * chunk, chunk), chunk)
            out[f, here, :] = wide[here, :].astype(jnp.bfloat16)
            return carry

        lax.fori_loop(0, columns // chunk, settle, 0)

    wait(rows.at[:, pl.ds(0, rows_y - own_rows)], in_send)
    wait(mixed.at[:, pl.ds(0, points_x - share_x), :], swap_send)
    wait(lowered.at[:, pl.ds(0, ncz - 1)], back_send)
    wait(landed.at[:, pl.ds(0, rows_y - own_rows)], out_send)


def on_device(nkx, ncz, field_modes, cotangent):
    local_k, fields, columns = field_modes.shape
    local_m = columns // Y
    modes_z, points_x = local_k * ncz, local_m * nkx
    own_rows = Y // nkx
    share_x = points_x // ncz
    bf16 = jnp.bfloat16
    pieces = next(p for p in (4, 3, 2, 1) if columns % (p * 128) == 0 or p == 1)

    cosines = cosine_table(MZ, modes_z)
    synthesis = (cosines * math.sqrt(2.0 / modes_z)).astype(bf16).T
    projection = (cosines * math.sqrt(2.0 / MZ)).astype(bf16).T
    hartley = hartley_table(points_x).astype(np.float32).astype(bf16)
    tables = jnp.asarray(np.concatenate([hartley, synthesis, projection], axis=0))

    hbm = pl.BlockSpec(memory_space=pltpu.HBM)
    dma = pltpu.SemaphoreType.DMA
    out = pl.pallas_call(
        functools.partial(kernel, nkx, ncz, pieces),
        out_shape=jax.ShapeDtypeStruct((fields, columns, local_k), bf16),
        in_specs=[hbm] * 3,
        out_specs=pl.BlockSpec(memory_space=pltpu.VMEM),
        scratch_shapes=[
            pltpu.VMEM((2, local_k, fields, columns), bf16),
            pltpu.VMEM(tables.shape, bf16),
            dma((2, pieces)), dma, pltpu.SemaphoreType.REGULAR((nkx // 2,)),
            pltpu.VMEM((columns, local_k), jnp.float32),
            pltpu.VMEM((2 * fields, Y, local_m, local_k), bf16),
            pltpu.VMEM((2 * fields, own_rows, points_x, local_k), bf16),
            pltpu.VMEM((2 * fields, points_x, own_rows * local_k), bf16),
            pltpu.VMEM((2 * fields, ncz, share_x, own_rows * local_k), bf16),
            pltpu.VMEM((fields, own_rows * share_x, MZ), jnp.float32),
            pltpu.VMEM((own_rows * share_x, MZ), jnp.float32),
            pltpu.VMEM((own_rows * share_x, MZ), bf16),
            pltpu.VMEM((fields, ncz, share_x, own_rows * local_k), bf16),
            pltpu.VMEM((fields, points_x, own_rows * local_k), bf16),
            pltpu.VMEM((fields, own_rows, points_x, local_k), bf16),
            pltpu.VMEM((fields, Y, local_m, local_k), bf16),
            dma, dma((2 * fields,)), dma, dma((2 * fields,)),
            dma, dma((fields,)), dma, dma((fields,)),
        ],
        compiler_params=pltpu.CompilerParams(has_side_effects=True, vmem_limit_bytes=52 * 2**20, collective_id=0),
    )(field_modes, cotangent, tables)
    return out.transpose(2, 0, 1)


def solution(mesh):
    return jax.shard_map(
        functools.partial(on_device, mesh.shape["kx"], mesh.shape["cz"]),
        mesh=mesh,
        in_specs=(P("cz", None, "kx"), P("cz", None, "kx")),
        out_specs=P("cz", None, "kx"),
        check_vma=False,
    )
```

time: 116 us -> 117 us (level)
  Pallas kernels: 111 us -> 114 us
  local copies, waits for them, and re-layouts: 4.89 us -> 2.46 us
    reshape x1 -> x0, local copies, waits for them, and re-layouts: 2.46 us -> none  [on_device(): return out.transpose(3, 1, 2, 0).reshape(local_k, fields, columns)]
    pallas_call x1, Pallas kernels: 111 us -> 114 us  [on_device(): pl.pallas_call(functools.partial(kernel, nkx, ncz, pieces), out_shape=jax...]
where the time goes in v1:
time: 117 us; the launch traced here: 116 us
  Pallas kernels  114 us (97%)
  local copies, waits for them, and re-layouts  2.46 us (2%)
    pallas_call x1, Pallas kernels, on_device(): pl.pallas_call(functools.partial(kernel, nkx, ncz, pieces), out_shape=jax...  114 us
    transpose x1, local copies, waits for them, and re-layouts, on_device(): return out.transpose(2, 0, 1)  2.46 us

profile of v1, /device:TPU:0, one launch (start us, length us, event | category | flops | bytes accessed | tf_op | source)
XLA Modules:
  0.0 116.2 jit_solution(1110450484672684585)
XLA Ops:
  0.0 113.8 %shard_map.37 = bf16[4,1536,128]{2,1,0:T(8,128)(2,1)S(1)} custom-call(bf16[128,4,1536]{2,1,0:T(4,128)(2,1)} %field_modes.1, bf16[128,4,1536]{2,1,0:T(4,128)(2,1)} %cotangent.1, bf16[1792,768]{1,0:T(8,128)(2,1)} %constant.2.clone.tables_in), custom_call_target="tpu_custom_call" | custom-call | tf_op jit(solution)/shard_map/pallas_call | solution.py:376
  113.8 2.5 %copy.4 = bf16[128,4,1536]{2,1,0:T(4,128)(2,1)} copy(bf16[128,4,1536]{0,2,1:T(8,128)(2,1)S(1)} %bitcast.1) | data formatting | bytes 3145728 | tf_op jit(solution)/shard_map/transpose | solution.py:402

commit v2 on v1

--- a/solution.py
+++ b/solution.py
@@ -51,11 +51,13 @@
     share_x = points_x // ncz
     aligned = local_k % 128 == 0
     i, j = lax.axis_index("kx"), lax.axis_index("cz")
+    ahead = 3
     order = ((0, 2), (1, 0), (1, 1), (1, 3), (0, 0), (0, 1), (0, 3), (1, 2))
 
     places = nkx // 2
     place, column = i // 2, lax.rem(i, 2)
     above, below = place + 1 < places, place > 0
+    inner = jnp.logical_or(place == places // 2 - 1, place == places // 2)
     near = 1 + jnp.where(above, 1, 0) + jnp.where(below, 1, 0)
 
     def at(row_owner, mode_owner):
@@ -143,12 +145,13 @@
         return target
 
     half = nkx // 2
-    steps = [s for s in range(1, half)] + [s for s in range(half, nkx) if s % 2] + [s for s in range(half, nkx) if not s % 2]
-
-    def others():
+    within = list(range(1, half))
+    across = [s for s in range(half, nkx) if s % 2] + [s for s in range(half, nkx) if not s % 2]
+
+    def targets(chosen):
         if nkx & (nkx - 1):
-            return [lax.rem(i + s, nkx) for s in range(1, nkx)]
-        return [flip(i, s) for s in steps]
+            return [lax.rem(i + s, nkx) for s in chosen]
+        return [flip(i, s) for s in chosen]
 
     def send_at_distance(h, distance):
         for hops, side in ((distance, 0), (distance - 1, 1)):
@@ -174,11 +177,16 @@
         send_at_distance(0, distance)
     keep_in(0)
     table_copy.start()
-    for h in range(1, 2 * fields):
-        prepare(h)
-        for target in others():
-            send_in(h, target)
-        keep_in(h)
+
+    def launch(h):
+        if h < 2 * fields:
+            prepare(h)
+            for target in targets(within + across):
+                send_in(h, target)
+            keep_in(h)
+
+    for h in range(1, ahead):
+        launch(h)
 
     def share_rows(q):
         return pl.ds(pl.multiple_of(q * share_x, share_x), share_x)
@@ -279,7 +287,10 @@
             result[f, r] = value
 
         transform(keep, [turned[f, :, lanes(r)] for r in range(own_rows)])
-        for target in others():
+        pltpu.make_async_copy(out_block(f, i), out_place(f), out_recv.at[f]).start()
+
+    def depart(f, chosen):
+        for target in targets(chosen):
             pltpu.make_async_remote_copy(
                 src_ref=out_block(f, target),
                 dst_ref=out_place(f),
@@ -288,7 +299,8 @@
                 device_id=at(target, j),
                 device_id_type=MESH,
             ).start()
-        pltpu.make_async_copy(out_block(f, i), out_place(f), out_recv.at[f]).start()
+
+    outer = jnp.logical_not(inner)
 
     def keep(h):
         def use(part, here, value):
@@ -314,29 +326,54 @@
 
     table_copy.wait()
     mix(0)
+    launch(ahead)
     mix(1)
+    launch(ahead + 1)
     lift(0, keep(0))
+    mix(2)
+    launch(ahead + 2)
     lift(1, keep_and_flux(1))
     leave(0)
-    mix(2)
-    finish(0)
+    mix(3)
+    launch(ahead + 3)
     lift(2, keep_and_flux(2))
     leave(1)
-    mix(3)
-    finish(1)
+    finish(0)
+    mix(4)
+    launch(ahead + 4)
     lift(3, keep_and_flux(3))
     leave(3)
-    mix(4)
+    finish(1)
+
+    @pl.when(inner)
+    def _():
+        depart(0, within + across)
+        depart(1, within + across)
+
+    mix(5)
+    launch(ahead + 5)
+    lift(4, first)
     finish(3)
-    lift(4, first)
-    mix(5)
+
+    @pl.when(inner)
+    def _():
+        depart(3, within + across)
+
+    mix(6)
+    launch(ahead + 6)
     lift(5, add(2))
-    mix(6)
+    mix(7)
+
+    @pl.when(outer)
+    def _():
+        for f in (0, 1, 3):
+            depart(f, within + across)
+
     lift(6, add(3))
-    mix(7)
     lift(7, last)
     leave(2)
     finish(2)
+    depart(2, within + across)
 
     for f in (0, 1, 3, 2):
         wait(landed.at[f], out_recv.at[f])

time: 117 us -> 112 us (0.957)
  Pallas kernels: 114 us -> 109 us
    pallas_call x1, Pallas kernels: 114 us -> 109 us  [on_device(): pl.pallas_call(functools.partial(kernel, nkx, ncz, pieces), out_shape=jax...]
where the time goes in v2:
time: 112 us
  Pallas kernels  109 us (97%)
  local copies, waits for them, and re-layouts  2.46 us (2%)
    pallas_call x1, Pallas kernels, on_device(): pl.pallas_call(functools.partial(kernel, nkx, ncz, pieces), out_shape=jax...  109 us
    transpose x1, local copies, waits for them, and re-layouts, on_device(): return out.transpose(2, 0, 1)  2.46 us

profile of v2, /device:TPU:0, one launch (start us, length us, event | category | flops | bytes accessed | tf_op | source)
XLA Modules:
  0.0 111.8 jit_solution(1757514841804419272)
XLA Ops:
  0.0 109.3 %shard_map.37 = bf16[4,1536,128]{2,1,0:T(8,128)(2,1)S(1)} custom-call(bf16[128,4,1536]{2,1,0:T(4,128)(2,1)} %field_modes.1, bf16[128,4,1536]{2,1,0:T(4,128)(2,1)} %cotangent.1, bf16[1792,768]{1,0:T(8,128)(2,1)} %constant.2.clone.tables_in), custom_call_target="tpu_custom_call" | custom-call | tf_op jit(solution)/shard_map/pallas_call | solution.py:413
  109.3 2.5 %copy.4 = bf16[128,4,1536]{2,1,0:T(4,128)(2,1)} copy(bf16[128,4,1536]{0,2,1:T(8,128)(2,1)S(1)} %bitcast.1) | data formatting | bytes 3145728 | tf_op jit(solution)/shard_map/transpose | solution.py:439

commit v3 on v2

--- a/solution.py
+++ b/solution.py
@@ -38,7 +38,7 @@
     field_modes, cotangent, tables_in,
     out,
     raw, tables, raw_sem, table_sem, ready,
-    wide, rows, held, mixed, parts, points, total, flux, lowered, turned, result, landed,
+    weave, wide, rows, held, mixed, parts, points, total, flux, lowered, turned, result, landed,
     in_send, in_recv, swap_send, swap_recv, back_send, back_recv, out_send, out_recv,
 ):
     local_k, fields, columns = field_modes.shape
@@ -95,37 +95,42 @@
     signal_near(barrier)
     for step in range(1, ncz):
         pl.semaphore_signal(barrier, inc=1, device_id=at(i, lax.rem(j + step, ncz)), device_id_type=MESH)
-    for copy in raw_copies[1]:
-        copy.start()
 
     hartley = tables.at[pl.ds(0, points_x)]
     lifts = [tables.at[pl.ds(points_x + n * modes_z, modes_z)] for n in range(2)]
-    chunk = 128 if piece % 128 == 0 else piece
-
-    def prepare(h):
+    group = 16
+    block = group * rows_y
+    row = lax.broadcasted_iota(jnp.int32, (block, block), 0)
+    lane = lax.broadcasted_iota(jnp.int32, (block, block), 1)
+    moved = lax.rem(row, group) * rows_y + row // group
+    weave[...] = jnp.where(moved == lane, 1.0, 0.0).astype(jnp.bfloat16)
+
+    def prepare(h, between=None):
         a, f = order[h]
 
         def turn(step, carry):
-            here = pl.ds(pl.multiple_of(step * chunk, chunk), chunk)
-            wide[here, :] = raw[a, :, f, here].astype(jnp.float32).T
+            here = pl.ds(pl.multiple_of(step * block, block), block)
+            value = matmul_t(weave[...], raw[a, :, f, here]).astype(jnp.bfloat16)
+            rows[h, :, pl.ds(pl.multiple_of(step * group, group), group), :] = value.reshape(rows_y, group, local_k)
             return carry
 
-        for p in range(pieces):
-            if h < 2:
+        if h >= 2:
+            lax.fori_loop(0, columns // block, turn, 0)
+        else:
+            span = columns // block // pieces
+            for p in range(pieces):
                 raw_copies[a][p].wait()
-                lax.fori_loop(p * (piece // chunk), (p + 1) * (piece // chunk), turn, 0)
-        if h >= 2:
-            lax.fori_loop(0, columns // chunk, turn, 0)
-        for y in range(rows_y):
-            rows[h, y] = wide[pl.ds(y, local_m, stride=rows_y), :].astype(jnp.bfloat16)
-
-    def in_place(h):
-        return held.at[h, :, pl.ds(pl.multiple_of(i * local_m, local_m), local_m)]
-
-    def send_in(h, target):
+                lax.fori_loop(p * span, (p + 1) * span, turn, 0)
+                if between is not None:
+                    between(p)
+
+    def in_place(h, start=0, count=local_m):
+        return held.at[h, :, pl.ds(pl.multiple_of(i * local_m, local_m) + start, count)]
+
+    def send_in(h, target, start=0, count=local_m):
         pltpu.make_async_remote_copy(
-            src_ref=rows.at[h, pl.ds(target * own_rows, own_rows)],
-            dst_ref=in_place(h),
+            src_ref=rows.at[h, pl.ds(target * own_rows, own_rows), pl.ds(start, count)],
+            dst_ref=in_place(h, start, count),
             send_sem=in_send,
             recv_sem=in_recv.at[h],
             device_id=at(target, j),
@@ -146,34 +151,44 @@
 
     half = nkx // 2
     within = list(range(1, half))
-    across = [s for s in range(half, nkx) if s % 2] + [s for s in range(half, nkx) if not s % 2]
+    across = [s for p in range(half // 2, places) for s in (2 * p + 1, 2 * p)]
 
     def targets(chosen):
         if nkx & (nkx - 1):
             return [lax.rem(i + s, nkx) for s in chosen]
         return [flip(i, s) for s in chosen]
 
-    def send_at_distance(h, distance):
+    def send_at_distance(h, distance, start=0, count=local_m):
         for hops, side in ((distance, 0), (distance - 1, 1)):
             facing = place * 2 + (column if side == 0 else 1 - column)
             if hops == 0:
-                send_in(h, facing)
+                send_in(h, facing, start, count)
             elif hops < places:
                 @pl.when(place + hops < places)
                 def _():
-                    send_in(h, facing + 2 * hops)
+                    send_in(h, facing + 2 * hops, start, count)
 
                 @pl.when(place >= hops)
                 def _():
-                    send_in(h, facing - 2 * hops)
-
-    prepare(0)
-    pl.semaphore_wait(barrier, near + ncz - 1)
-    send_at_distance(0, 1)
+                    send_in(h, facing - 2 * hops, start, count)
+
+    part_m = local_m // pieces
+
+    def begin(p):
+        if p == 0:
+            pl.semaphore_wait(barrier, near + ncz - 1)
+            if places > 1:
+                signal_near(ready.at[0])
+        if p == pieces - 1:
+            for copy in raw_copies[1]:
+                copy.start()
+        send_at_distance(0, 1, p * part_m, part_m)
+
+    prepare(0, begin)
     for distance in range(2, places + 1):
-        sem = ready.at[distance - 2]
-        signal_near(sem)
-        pl.semaphore_wait(sem, near)
+        pl.semaphore_wait(ready.at[distance - 2], near)
+        if distance < places:
+            signal_near(ready.at[distance - 1])
         send_at_distance(0, distance)
     keep_in(0)
     table_copy.start()
@@ -287,7 +302,7 @@
             result[f, r] = value
 
         transform(keep, [turned[f, :, lanes(r)] for r in range(own_rows)])
-        pltpu.make_async_copy(out_block(f, i), out_place(f), out_recv.at[f]).start()
+        pltpu.make_async_copy(out_block(f, i), out_place(f), out_recv.at[f, i]).start()
 
     def depart(f, chosen):
         for target in targets(chosen):
@@ -295,7 +310,7 @@
                 src_ref=out_block(f, target),
                 dst_ref=out_place(f),
                 send_sem=out_send,
-                recv_sem=out_recv.at[f],
+                recv_sem=out_recv.at[f, i],
                 device_id=at(target, j),
                 device_id_type=MESH,
             ).start()
@@ -375,10 +390,14 @@
     finish(2)
     depart(2, within + across)
 
+    chunk = 128 if columns % 128 == 0 else columns
     for f in (0, 1, 3, 2):
-        wait(landed.at[f], out_recv.at[f])
-        for y in range(rows_y):
-            wide[pl.ds(y, local_m, stride=rows_y), :] = landed[f, y].astype(jnp.float32)
+        for step in [0] + within + across:
+            source = targets([step])[0]
+            wait(landed.at[f, pl.ds(source * own_rows, own_rows)], out_recv.at[f, source])
+            for r in range(own_rows):
+                y = source * own_rows + r
+                wide[pl.ds(y, local_m, stride=rows_y), :] = landed[f, y].astype(jnp.float32)
 
         def settle(step, carry):
             here = pl.ds(pl.multiple_of(step * chunk, chunk), chunk)
@@ -400,7 +419,7 @@
     own_rows = Y // nkx
     share_x = points_x // ncz
     bf16 = jnp.bfloat16
-    pieces = next(p for p in (4, 3, 2, 1) if columns % (p * 128) == 0 or p == 1)
+    pieces = next(p for p in (3, 2, 1) if columns % (p * 16 * Y) == 0 or p == 1)
 
     cosines = cosine_table(MZ, modes_z)
     synthesis = (cosines * math.sqrt(2.0 / modes_z)).astype(bf16).T
@@ -419,6 +438,7 @@
             pltpu.VMEM((2, local_k, fields, columns), bf16),
             pltpu.VMEM(tables.shape, bf16),
             dma((2, pieces)), dma, pltpu.SemaphoreType.REGULAR((nkx // 2,)),
+            pltpu.VMEM((16 * Y, 16 * Y), bf16),
             pltpu.VMEM((columns, local_k), jnp.float32),
             pltpu.VMEM((2 * fields, Y, local_m, local_k), bf16),
             pltpu.VMEM((2 * fields, own_rows, points_x, local_k), bf16),
@@ -432,7 +452,7 @@
             pltpu.VMEM((fields, own_rows, points_x, local_k), bf16),
             pltpu.VMEM((fields, Y, local_m, local_k), bf16),
             dma, dma((2 * fields,)), dma, dma((2 * fields,)),
-            dma, dma((fields,)), dma, dma((fields,)),
+            dma, dma((fields,)), dma, dma((fields, nkx)),
         ],
         compiler_params=pltpu.CompilerParams(has_side_effects=True, vmem_limit_bytes=52 * 2**20, collective_id=0),
     )(field_modes, cotangent, tables)

time: 112 us -> 110 us (0.982)
    pallas_call x1, Pallas kernels: 109 us -> 108 us  [on_device(): pl.pallas_call(functools.partial(kernel, nkx, ncz, pieces), out_shape=jax...]
where the time goes in v3:
time: 110 us
  Pallas kernels  108 us (98%)
  local copies, waits for them, and re-layouts  2.46 us (2%)
    pallas_call x1, Pallas kernels, on_device(): pl.pallas_call(functools.partial(kernel, nkx, ncz, pieces), out_shape=jax...  108 us
    transpose x1, local copies, waits for them, and re-layouts, on_device(): return out.transpose(2, 0, 1)  2.46 us

profile of v3, /device:TPU:0, one launch (start us, length us, event | category | flops | bytes accessed | tf_op | source)
XLA Modules:
  0.0 110.2 jit_solution(1926693599386293510)
XLA Ops:
  0.0 107.7 %shard_map.37 = bf16[4,1536,128]{2,1,0:T(8,128)(2,1)S(1)} custom-call(bf16[128,4,1536]{2,1,0:T(4,128)(2,1)} %field_modes.1, bf16[128,4,1536]{2,1,0:T(4,128)(2,1)} %cotangent.1, bf16[1792,768]{1,0:T(8,128)(2,1)} %constant.2.clone.tables_in), custom_call_target="tpu_custom_call" | custom-call | tf_op jit(solution)/shard_map/pallas_call | solution.py:432
  107.7 2.5 %copy.4 = bf16[128,4,1536]{2,1,0:T(4,128)(2,1)} copy(bf16[128,4,1536]{0,2,1:T(8,128)(2,1)S(1)} %bitcast.1) | data formatting | bytes 3145728 | tf_op jit(solution)/shard_map/transpose | solution.py:459

commit v4 on v3

--- a/solution.py
+++ b/solution.py
@@ -38,7 +38,7 @@
     field_modes, cotangent, tables_in,
     out,
     raw, tables, raw_sem, table_sem, ready,
-    weave, wide, rows, held, mixed, parts, points, total, flux, lowered, turned, result, landed,
+    weave, wide, stage, rows, held, mixed, parts, points, total, flux, lowered, turned, result, landed,
     in_send, in_recv, swap_send, swap_recv, back_send, back_recv, out_send, out_recv,
 ):
     local_k, fields, columns = field_modes.shape
@@ -98,7 +98,7 @@
 
     hartley = tables.at[pl.ds(0, points_x)]
     lifts = [tables.at[pl.ds(points_x + n * modes_z, modes_z)] for n in range(2)]
-    group = 16
+    chunk, group = 128, 16
     block = group * rows_y
     row = lax.broadcasted_iota(jnp.int32, (block, block), 0)
     lane = lax.broadcasted_iota(jnp.int32, (block, block), 1)
@@ -302,7 +302,7 @@
             result[f, r] = value
 
         transform(keep, [turned[f, :, lanes(r)] for r in range(own_rows)])
-        pltpu.make_async_copy(out_block(f, i), out_place(f), out_recv.at[f, i]).start()
+        pltpu.make_async_copy(out_block(f, i), out_place(f), out_recv.at[f]).start()
 
     def depart(f, chosen):
         for target in targets(chosen):
@@ -310,12 +310,26 @@
                 src_ref=out_block(f, target),
                 dst_ref=out_place(f),
                 send_sem=out_send,
-                recv_sem=out_recv.at[f, i],
+                recv_sem=out_recv.at[f],
                 device_id=at(target, j),
                 device_id_type=MESH,
             ).start()
 
     outer = jnp.logical_not(inner)
+
+    def settle(f):
+        wait(landed.at[f], out_recv.at[f])
+        for y in range(rows_y):
+            wide[pl.ds(y, local_m, stride=rows_y), :] = landed[f, y].astype(jnp.float32)
+
+        def lay(step, carry):
+            here = pl.ds(pl.multiple_of(step * chunk, chunk), chunk)
+            stage[step, pl.ds(f, local_k, stride=fields), :] = wide[here, :].T
+            if f == 2:
+                out[step] = stage[step].astype(jnp.bfloat16)
+            return carry
+
+        lax.fori_loop(0, columns // chunk, lay, 0, unroll=f in (2, 3))
 
     def keep(h):
         def use(part, here, value):
@@ -390,26 +404,19 @@
     finish(2)
     depart(2, within + across)
 
-    chunk = 128 if columns % 128 == 0 else columns
     for f in (0, 1, 3, 2):
-        for step in [0] + within + across:
-            source = targets([step])[0]
-            wait(landed.at[f, pl.ds(source * own_rows, own_rows)], out_recv.at[f, source])
-            for r in range(own_rows):
-                y = source * own_rows + r
-                wide[pl.ds(y, local_m, stride=rows_y), :] = landed[f, y].astype(jnp.float32)
-
-        def settle(step, carry):
-            here = pl.ds(pl.multiple_of(step * chunk, chunk), chunk)
-            out[f, here, :] = wide[here, :].astype(jnp.bfloat16)
-            return carry
-
-        lax.fori_loop(0, columns // chunk, settle, 0)
+        settle(f)
 
     wait(rows.at[:, pl.ds(0, rows_y - own_rows)], in_send)
     wait(mixed.at[:, pl.ds(0, points_x - share_x), :], swap_send)
     wait(lowered.at[:, pl.ds(0, ncz - 1)], back_send)
     wait(landed.at[:, pl.ds(0, rows_y - own_rows)], out_send)
+
+
+def deliver(tiles, out, sem):
+    for n in range(tiles.shape[0]):
+        pltpu.make_async_copy(tiles.at[n], out.at[:, :, pl.ds(n * 128, 128)], sem).start()
+    pltpu.make_async_copy(out, out, sem).wait()
 
 
 def on_device(nkx, ncz, field_modes, cotangent):
@@ -431,7 +438,7 @@
     dma = pltpu.SemaphoreType.DMA
     out = pl.pallas_call(
         functools.partial(kernel, nkx, ncz, pieces),
-        out_shape=jax.ShapeDtypeStruct((fields, columns, local_k), bf16),
+        out_shape=jax.ShapeDtypeStruct((columns // 128, fields * local_k, 128), bf16),
         in_specs=[hbm] * 3,
         out_specs=pl.BlockSpec(memory_space=pltpu.VMEM),
         scratch_shapes=[
@@ -440,6 +447,7 @@
             dma((2, pieces)), dma, pltpu.SemaphoreType.REGULAR((nkx // 2,)),
             pltpu.VMEM((16 * Y, 16 * Y), bf16),
             pltpu.VMEM((columns, local_k), jnp.float32),
+            pltpu.VMEM((columns // 128, fields * local_k, 128), jnp.float32),
             pltpu.VMEM((2 * fields, Y, local_m, local_k), bf16),
             pltpu.VMEM((2 * fields, own_rows, points_x, local_k), bf16),
             pltpu.VMEM((2 * fields, points_x, own_rows * local_k), bf16),
@@ -452,11 +460,18 @@
             pltpu.VMEM((fields, own_rows, points_x, local_k), bf16),
             pltpu.VMEM((fields, Y, local_m, local_k), bf16),
             dma, dma((2 * fields,)), dma, dma((2 * fields,)),
-            dma, dma((fields,)), dma, dma((fields, nkx)),
+            dma, dma((fields,)), dma, dma((fields,)),
         ],
         compiler_params=pltpu.CompilerParams(has_side_effects=True, vmem_limit_bytes=52 * 2**20, collective_id=0),
     )(field_modes, cotangent, tables)
-    return out.transpose(2, 0, 1)
+    return pl.pallas_call(
+        deliver,
+        out_shape=jax.ShapeDtypeStruct(field_modes.shape, bf16),
+        in_specs=[pl.BlockSpec(memory_space=pl.ANY)],
+        out_specs=hbm,
+        scratch_shapes=[dma],
+        compiler_params=pltpu.CompilerParams(vmem_limit_bytes=2 * 2**20),
+    )(out.reshape(columns // 128, local_k, fields, 128))
 
 
 def solution(mesh):

time: 110 us -> 109 us (level)
  local copies, waits for them, and re-layouts: 2.46 us -> 0 us
    transpose x1 -> x0, local copies, waits for them, and re-layouts: 2.46 us -> none  [on_device(): return out.transpose(2, 0, 1)]
    pallas_call x0 -> x1, Pallas kernels: none -> 1.14 us  [on_device(): pl.pallas_call(deliver, out_shape=jax.ShapeDtypeStruct(field_modes.shape,...]
where the time goes in v4:
time: 109 us
  Pallas kernels  109 us (100%)
    pallas_call x1, Pallas kernels, on_device(): pl.pallas_call(functools.partial(kernel, nkx, ncz, pieces), out_shape=jax...  108 us

profile of v4, /device:TPU:0, one launch (start us, length us, event | category | flops | bytes accessed | tf_op | source)
XLA Modules:
  0.0 109.1 jit_solution(18425202453385541440)
XLA Ops:
  0.0 107.7 %shard_map.37 = bf16[12,512,128]{2,1,0:T(8,128)(2,1)S(1)} custom-call(bf16[128,4,1536]{2,1,0:T(4,128)(2,1)} %field_modes.1, bf16[128,4,1536]{2,1,0:T(4,128)(2,1)} %cotangent.1, bf16[1792,768]{1,0:T(8,128)(2,1)} %constant.2.clone.tables_in), custom_call_target="tpu_custom_call" | custom-call | tf_op jit(solution)/shard_map/pallas_call | solution.py:439
  107.8 1.1 %shard_map.38 = bf16[128,4,1536]{2,1,0:T(4,128)(2,1)} custom-call(bf16[12,128,4,128]{3,2,1,0:T(4,128)(2,1)S(1)} %bitcast.1), custom_call_target="tpu_custom_call" | custom-call | tf_op jit(solution)/shard_map/pallas_call | solution.py:467

commit v5 on v4

--- a/solution.py
+++ b/solution.py
@@ -413,6 +413,300 @@
     wait(landed.at[:, pl.ds(0, rows_y - own_rows)], out_send)
 
 
+def kernel_halves(
+    nkx, ncz, pieces,
+    field_modes, cotangent, tables_in,
+    out,
+    raw, tables, raw_sem, table_sem, ready,
+    weave, wide, stage, rows, held, kept, mixed, vertical, other, total, flux, lowered, result, beyond, landed, crossed,
+    in_send, in_recv, out_send, out_recv, cross_recv,
+):
+    local_k, fields, columns = field_modes.shape
+    rows_y = rows.shape[1]
+    local_m = columns // rows_y
+    points_x = local_m * nkx
+    points_z = vertical.shape[1]
+    modes_z = local_k * ncz
+    members = nkx // 2
+    half_m = members * local_m
+    i, j = lax.axis_index("kx"), lax.axis_index("cz")
+    side, member = i // members, lax.rem(i, members)
+    my_row = member * ncz + j
+    order = ((0, 2), (0, 0), (1, 0), (0, 1), (1, 1), (0, 3), (1, 3), (1, 2))
+    shared = (True, False) * fields
+    ahead = 4
+
+    places = nkx // 2
+    place, column = i // 2, lax.rem(i, 2)
+    above, below = place + 1 < places, place > 0
+    near = ncz + jnp.where(above, 1, 0) + jnp.where(below, 1, 0)
+
+    def at(row_owner, mode_owner):
+        return {"kx": row_owner, "cz": mode_owner}
+
+    def wait(ref, sem):
+        pltpu.make_async_copy(ref, ref, sem).wait()
+
+    piece = columns // pieces
+    raw_copies = [
+        [
+            pltpu.make_async_copy(
+                array.at[:, :, pl.ds(p * piece, piece)], raw.at[a, :, :, pl.ds(p * piece, piece)], raw_sem.at[a, p]
+            )
+            for p in range(pieces)
+        ]
+        for a, array in enumerate((field_modes, cotangent))
+    ]
+    table_copy = pltpu.make_async_copy(tables_in, tables, table_sem)
+    for copy in raw_copies[0]:
+        copy.start()
+    barrier = pltpu.get_barrier_semaphore()
+
+    def signal_near(sem):
+        pl.semaphore_signal(sem, inc=1, device_id=at(place * 2 + 1 - column, j), device_id_type=MESH)
+
+        @pl.when(above)
+        def _():
+            pl.semaphore_signal(sem, inc=1, device_id=at(i + 2, j), device_id_type=MESH)
+
+        @pl.when(below)
+        def _():
+            pl.semaphore_signal(sem, inc=1, device_id=at(i - 2, j), device_id_type=MESH)
+
+        for step in range(1, ncz):
+            pl.semaphore_signal(sem, inc=1, device_id=at(i, lax.rem(j + step, ncz)), device_id_type=MESH)
+
+    signal_near(barrier)
+    hartley = tables.at[pl.ds(0, points_x)]
+    lifts = [tables.at[pl.ds(points_x + n * modes_z, modes_z)] for n in range(2)]
+    chunk, group = 128, 16
+    block = group * rows_y
+    row = lax.broadcasted_iota(jnp.int32, (block, block), 0)
+    lane = lax.broadcasted_iota(jnp.int32, (block, block), 1)
+    moved = lax.rem(row, group) * rows_y + row // group
+    weave[...] = jnp.where(moved == lane, 1.0, 0.0).astype(jnp.bfloat16)
+
+    def prepare(h, between=None):
+        a, f = order[h]
+
+        def turn(step, carry):
+            here = pl.ds(pl.multiple_of(step * block, block), block)
+            value = matmul_t(weave[...], raw[a, :, f, here]).astype(jnp.bfloat16)
+            rows[h, :, pl.ds(pl.multiple_of(step * group, group), group), :] = value.reshape(rows_y, group, local_k)
+            return carry
+
+        if all(order[n][0] != a for n in range(h)):
+            span = columns // block // pieces
+            for p in range(pieces):
+                raw_copies[a][p].wait()
+                lax.fori_loop(p * span, (p + 1) * span, turn, 0)
+                if between is not None:
+                    between(p)
+        else:
+            lax.fori_loop(0, columns // block, turn, 0)
+
+    my_lanes = pl.ds(pl.multiple_of(j * local_k, local_k), local_k)
+
+    def in_place(h, start=0, count=local_m):
+        if shared[h]:
+            return held.at[h // 2, pl.ds(pl.multiple_of(i * local_m, local_m) + start, count), my_lanes]
+        return kept.at[h // 2, pl.ds(pl.multiple_of(member * local_m, local_m) + start, count), my_lanes]
+
+    def send_in(h, row_owner, mode_owner, start=0, count=local_m):
+        pltpu.make_async_remote_copy(
+            src_ref=rows.at[h, lax.rem(row_owner, members) * ncz + mode_owner, pl.ds(start, count)],
+            dst_ref=in_place(h, start, count),
+            send_sem=in_send,
+            recv_sem=in_recv.at[h],
+            device_id=at(row_owner, mode_owner),
+            device_id_type=MESH,
+        ).start()
+
+    def keep_in(h):
+        pltpu.make_async_copy(rows.at[h, my_row], in_place(h), in_recv.at[h]).start()
+
+    def flip(index, step):
+        bit = 1
+        target = index
+        while bit < nkx:
+            if step & bit:
+                target = target + bit * (1 - 2 * lax.rem(index // bit, 2))
+            bit *= 2
+        return target
+
+    within = list(range(1, members))
+    across = [s for p in range(members // 2, places) for s in (2 * p + 1, 2 * p)]
+
+    def to_all(steps, send):
+        for s in steps:
+            target = flip(i, s)
+
+            def one(step, carry):
+                send(target, lax.rem(j + step, ncz))
+                return carry
+
+            lax.fori_loop(0 if s else 1, ncz, one, 0)
+
+    def hop_away(hops, side_step, use):
+        facing = place * 2 + (1 - column if side_step else column)
+        if hops == 0:
+            use(facing)
+        elif hops < places:
+            @pl.when(place + hops < places)
+            def _():
+                use(facing + 2 * hops)
+
+            @pl.when(place >= hops)
+            def _():
+                use(facing - 2 * hops)
+
+    def each_other(send, target):
+        def one(step, carry):
+            send(target, lax.rem(j + step, ncz))
+            return carry
+
+        lax.fori_loop(1, ncz, one, 0)
+
+    part_m = local_m // pieces
+
+    def begin(p):
+        if p == 0:
+            pl.semaphore_wait(barrier, near)
+            signal_near(ready.at[0])
+        if p == pieces - 1:
+            for copy in raw_copies[1]:
+                copy.start()
+        hop_away(1, False, lambda t: send_in(0, t, j, p * part_m, part_m))
+        hop_away(0, True, lambda t: send_in(0, t, j, p * part_m, part_m))
+
+    prepare(0, begin)
+    send_0 = functools.partial(send_in, 0)
+    each_other(send_0, i)
+    for distance in range(2, places + 2):
+        pl.semaphore_wait(ready.at[distance - 2], near)
+        if distance < places + 1:
+            signal_near(ready.at[distance - 1])
+        if distance <= places:
+            hop_away(distance, False, lambda t: send_in(0, t, j))
+            hop_away(distance - 1, True, lambda t: send_in(0, t, j))
+        hop_away(distance - 1, False, lambda t: each_other(send_0, t))
+        hop_away(distance - 2, True, lambda t: each_other(send_0, t))
+    keep_in(0)
+    table_copy.start()
+
+    def launch(h):
+        if h < 2 * fields:
+            prepare(h)
+            to_all([0] + within + (across if shared[h] else []), functools.partial(send_in, h))
+            keep_in(h)
+
+    for h in range(1, ahead):
+        launch(h)
+
+    half_lanes = modes_z // 2
+    parts = [slice(n * half_lanes, (n + 1) * half_lanes) for n in range(2)]
+    block_z = 256 if points_z % 256 == 0 else points_z
+
+    def own_m(which):
+        return pl.ds(pl.multiple_of(which * half_m, half_m), half_m)
+
+    def gather(h, use):
+        source = held.at[h // 2] if shared[h] else kept.at[h // 2]
+        wait(source, in_recv.at[h])
+        for part in parts:
+            table = hartley[...] if shared[h] else hartley[:, own_m(side)]
+            mixed[:, part] = matmul(table, source[:, part]).astype(jnp.bfloat16)
+        launch(h + ahead)
+        lift_table = lifts[order[h][0]]
+
+        def one(step, carry):
+            here = pl.ds(pl.multiple_of(step * block_z, block_z), block_z)
+            use(here, matmul(mixed[...], lift_table[:, here]))
+            return carry
+
+        lax.fori_loop(0, points_z // block_z, one, 0)
+
+    def lower():
+        for part in parts:
+            lowered[:, part] = matmul_t(flux[...], lifts[0][part, :]).astype(jnp.bfloat16)
+
+    def out_block(ref, row_owner, mode_owner):
+        first_m = pl.multiple_of(lax.rem(row_owner, members) * local_m, local_m)
+        return ref.at[pl.ds(first_m, local_m), pl.ds(pl.multiple_of(mode_owner * local_k, local_k), local_k)]
+
+    def send_out(source, target, sem, row_owner, mode_owner):
+        pltpu.make_async_remote_copy(
+            src_ref=out_block(source, row_owner, mode_owner),
+            dst_ref=target,
+            send_sem=out_send,
+            recv_sem=sem,
+            device_id=at(row_owner, mode_owner),
+            device_id_type=MESH,
+        ).start()
+
+    def finish(f):
+        lower()
+        if f == 2:
+            for part in parts:
+                beyond[:, part] = matmul(hartley[own_m(1 - side), :], lowered[:, part]).astype(jnp.bfloat16)
+            to_all(across, functools.partial(send_out, beyond, crossed.at[my_row], cross_recv))
+        for part in parts:
+            result[f, :, part] = matmul(hartley[own_m(side), :], lowered[:, part]).astype(jnp.bfloat16)
+        pltpu.make_async_copy(out_block(result.at[f], i, j), landed.at[f, my_row], out_recv.at[f]).start()
+        to_all([0] + within, functools.partial(send_out, result.at[f], landed.at[f, my_row], out_recv.at[f]))
+
+    def keep(target):
+        def use(here, value):
+            target[:, here] = value
+        return use
+
+    def multiply(first):
+        def use(here, value):
+            flux[:, here] = (value * vertical[:, here]).astype(jnp.bfloat16)
+            product = value * other[:, here]
+            total[:, here] = product if first else total[:, here] + product
+        return use
+
+    def last(here, value):
+        flux[:, here] = (total[:, here] + 2.0 * value * vertical[:, here]).astype(jnp.bfloat16)
+
+    table_copy.wait()
+    gather(0, keep(vertical))
+    for h, f in ((1, 0), (3, 1), (5, 3)):
+        gather(h, keep(other))
+        gather(h + 1, multiply(h == 1))
+        finish(f)
+    gather(7, last)
+    finish(2)
+
+    def settle(f):
+        wait(landed.at[f], out_recv.at[f])
+        if f == 2:
+            wait(crossed, cross_recv)
+        for y in range(rows_y):
+            value = landed[f, y].astype(jnp.float32)
+            if f == 2:
+                value += crossed[y].astype(jnp.float32)
+            wide[pl.ds(y, local_m, stride=rows_y), :] = value
+
+        def lay(step, carry):
+            here = pl.ds(pl.multiple_of(step * chunk, chunk), chunk)
+            stage[step, pl.ds(f, local_k, stride=fields), :] = wide[here, :].T
+            if f == 2:
+                out[step] = stage[step].astype(jnp.bfloat16)
+            return carry
+
+        lax.fori_loop(0, columns // chunk, lay, 0, unroll=f == 2)
+
+    for f in (0, 1, 3, 2):
+        settle(f)
+
+    wait(rows.at[pl.ds(0, fields)], in_send)
+    wait(rows.at[:, pl.ds(0, rows_y - 1)], in_send)
+    wait(landed.at[:, pl.ds(0, rows_y - 1)], out_send)
+    wait(crossed, out_send)
+
+
 def deliver(tiles, out, sem):
     for n in range(tiles.shape[0]):
         pltpu.make_async_copy(tiles.at[n], out.at[:, :, pl.ds(n * 128, 128)], sem).start()
@@ -436,19 +730,28 @@
 
     hbm = pl.BlockSpec(memory_space=pltpu.HBM)
     dma = pltpu.SemaphoreType.DMA
-    out = pl.pallas_call(
-        functools.partial(kernel, nkx, ncz, pieces),
-        out_shape=jax.ShapeDtypeStruct((columns // 128, fields * local_k, 128), bf16),
-        in_specs=[hbm] * 3,
-        out_specs=pl.BlockSpec(memory_space=pltpu.VMEM),
-        scratch_shapes=[
-            pltpu.VMEM((2, local_k, fields, columns), bf16),
-            pltpu.VMEM(tables.shape, bf16),
-            dma((2, pieces)), dma, pltpu.SemaphoreType.REGULAR((nkx // 2,)),
-            pltpu.VMEM((16 * Y, 16 * Y), bf16),
-            pltpu.VMEM((columns, local_k), jnp.float32),
-            pltpu.VMEM((columns // 128, fields * local_k, 128), jnp.float32),
-            pltpu.VMEM((2 * fields, Y, local_m, local_k), bf16),
+    whole_rows = nkx // 2 * ncz == Y and nkx & (nkx - 1) == 0 and local_k % 128 == 0
+    if whole_rows:
+        members = nkx // 2
+        body = kernel_halves
+        scratch = [
+            pltpu.VMEM((fields, points_x, modes_z), bf16),
+            pltpu.VMEM((fields, members * local_m, modes_z), bf16),
+            pltpu.VMEM((points_x, modes_z), bf16),
+            pltpu.VMEM((points_x, MZ), jnp.float32),
+            pltpu.VMEM((points_x, MZ), jnp.float32),
+            pltpu.VMEM((points_x, MZ), jnp.float32),
+            pltpu.VMEM((points_x, MZ), bf16),
+            pltpu.VMEM((points_x, modes_z), bf16),
+            pltpu.VMEM((fields, members * local_m, modes_z), bf16),
+            pltpu.VMEM((members * local_m, modes_z), bf16),
+            pltpu.VMEM((fields, Y, local_m, local_k), bf16),
+            pltpu.VMEM((Y, local_m, local_k), bf16),
+            dma, dma((2 * fields,)), dma, dma((fields,)), dma,
+        ]
+    else:
+        body = kernel
+        scratch = [
             pltpu.VMEM((2 * fields, own_rows, points_x, local_k), bf16),
             pltpu.VMEM((2 * fields, points_x, own_rows * local_k), bf16),
             pltpu.VMEM((2 * fields, ncz, share_x, own_rows * local_k), bf16),
@@ -461,6 +764,21 @@
             pltpu.VMEM((fields, Y, local_m, local_k), bf16),
             dma, dma((2 * fields,)), dma, dma((2 * fields,)),
             dma, dma((fields,)), dma, dma((fields,)),
+        ]
+    out = pl.pallas_call(
+        functools.partial(body, nkx, ncz, pieces),
+        out_shape=jax.ShapeDtypeStruct((columns // 128, fields * local_k, 128), bf16),
+        in_specs=[hbm] * 3,
+        out_specs=pl.BlockSpec(memory_space=pltpu.VMEM),
+        scratch_shapes=[
+            pltpu.VMEM((2, local_k, fields, columns), bf16),
+            pltpu.VMEM(tables.shape, bf16),
+            dma((2, pieces)), dma, pltpu.SemaphoreType.REGULAR((nkx // 2 + 1,)),
+            pltpu.VMEM((16 * Y, 16 * Y), bf16),
+            pltpu.VMEM((columns, local_k), jnp.float32),
+            pltpu.VMEM((columns // 128, fields * local_k, 128), jnp.float32),
+            pltpu.VMEM((2 * fields, Y, local_m, local_k), bf16),
+            *scratch,
         ],
         compiler_params=pltpu.CompilerParams(has_side_effects=True, vmem_limit_bytes=52 * 2**20, collective_id=0),
     )(field_modes, cotangent, tables)

time: 109 us -> 104 us (0.954)
  Pallas kernels: 109 us -> 103 us
    pallas_call x1, Pallas kernels: 108 us -> 102 us  [on_device(): pl.pallas_call(functools.partial(body, nkx, ncz, pieces), out_shape=jax.S...]
where the time goes in v5:
time: 104 us; the launch traced here: 103 us
  Pallas kernels  103 us (99%)
    pallas_call x1, Pallas kernels, on_device(): pl.pallas_call(functools.partial(body, nkx, ncz, pieces), out_shape=jax.S...  102 us

profile of v5, /device:TPU:0, one launch (start us, length us, event | category | flops | bytes accessed | tf_op | source)
XLA Modules:
  0.0 103.0 jit_solution(5820155593716452063)
XLA Ops:
  0.0 101.9 %shard_map.37 = bf16[12,512,128]{2,1,0:T(8,128)(2,1)S(1)} custom-call(bf16[128,4,1536]{2,1,0:T(4,128)(2,1)} %field_modes.1, bf16[128,4,1536]{2,1,0:T(4,128)(2,1)} %cotangent.1, bf16[1792,768]{1,0:T(8,128)(2,1)} %constant.2.clone.tables_in), custom_call_target="tpu_custom_call" | custom-call | tf_op jit(solution)/shard_map/pallas_call | solution.py:768
  101.9 1.1 %shard_map.38 = bf16[128,4,1536]{2,1,0:T(4,128)(2,1)} custom-call(bf16[12,128,4,128]{3,2,1,0:T(4,128)(2,1)S(1)} %bitcast.1), custom_call_target="tpu_custom_call" | custom-call | tf_op jit(solution)/shard_map/pallas_call | solution.py:785

commit v6 on v5

--- a/solution.py
+++ b/solution.py
@@ -418,7 +418,7 @@
     field_modes, cotangent, tables_in,
     out,
     raw, tables, raw_sem, table_sem, ready,
-    weave, wide, stage, rows, held, kept, mixed, vertical, other, total, flux, lowered, result, beyond, landed, crossed,
+    weave, wide, stage, rows, held, kept, mixed, vertical, other, total, flux, summed, lowered, result, beyond, landed, crossed,
     in_send, in_recv, out_send, out_recv, cross_recv,
 ):
     local_k, fields, columns = field_modes.shape
@@ -432,9 +432,10 @@
     i, j = lax.axis_index("kx"), lax.axis_index("cz")
     side, member = i // members, lax.rem(i, members)
     my_row = member * ncz + j
-    order = ((0, 2), (0, 0), (1, 0), (0, 1), (1, 1), (0, 3), (1, 3), (1, 2))
-    shared = (True, False) * fields
-    ahead = 4
+    order = ((0, 2), (0, 0), (1, 0), (0, 1), (1, 1), (0, 3), (1, 2), (1, 3))
+    shared = (True, False, True, False, True, False, False, True)
+    place_of = [sum(shared[:h]) if shared[h] else h - sum(shared[:h]) for h in range(2 * fields)]
+    ahead = 6
 
     places = nkx // 2
     place, column = i // 2, lax.rem(i, 2)
@@ -509,8 +510,8 @@
 
     def in_place(h, start=0, count=local_m):
         if shared[h]:
-            return held.at[h // 2, pl.ds(pl.multiple_of(i * local_m, local_m) + start, count), my_lanes]
-        return kept.at[h // 2, pl.ds(pl.multiple_of(member * local_m, local_m) + start, count), my_lanes]
+            return held.at[place_of[h], pl.ds(pl.multiple_of(i * local_m, local_m) + start, count), my_lanes]
+        return kept.at[place_of[h], pl.ds(pl.multiple_of(member * local_m, local_m) + start, count), my_lanes]
 
     def send_in(h, row_owner, mode_owner, start=0, count=local_m):
         pltpu.make_async_remote_copy(
@@ -538,14 +539,17 @@
     across = [s for p in range(members // 2, places) for s in (2 * p + 1, 2 * p)]
 
     def to_all(steps, send):
-        for s in steps:
-            target = flip(i, s)
-
-            def one(step, carry):
-                send(target, lax.rem(j + step, ncz))
-                return carry
-
-            lax.fori_loop(0 if s else 1, ncz, one, 0)
+        def one(step, carry):
+            for s in steps:
+                if s:
+                    send(flip(i, s), lax.rem(j + step, ncz))
+                else:
+                    @pl.when(step > 0)
+                    def _():
+                        send(i, lax.rem(j + step, ncz))
+            return carry
+
+        lax.fori_loop(0, ncz, one, 0)
 
     def hop_away(hops, side_step, use):
         facing = place * 2 + (1 - column if side_step else column)
@@ -611,7 +615,7 @@
         return pl.ds(pl.multiple_of(which * half_m, half_m), half_m)
 
     def gather(h, use):
-        source = held.at[h // 2] if shared[h] else kept.at[h // 2]
+        source = held.at[place_of[h]] if shared[h] else kept.at[place_of[h]]
         wait(source, in_recv.at[h])
         for part in parts:
             table = hartley[...] if shared[h] else hartley[:, own_m(side)]
@@ -626,9 +630,9 @@
 
         lax.fori_loop(0, points_z // block_z, one, 0)
 
-    def lower():
+    def lower(source):
         for part in parts:
-            lowered[:, part] = matmul_t(flux[...], lifts[0][part, :]).astype(jnp.bfloat16)
+            lowered[:, part] = matmul_t(source[...], lifts[0][part, :]).astype(jnp.bfloat16)
 
     def out_block(ref, row_owner, mode_owner):
         first_m = pl.multiple_of(lax.rem(row_owner, members) * local_m, local_m)
@@ -645,7 +649,7 @@
         ).start()
 
     def finish(f):
-        lower()
+        lower(summed if f == 2 else flux)
         if f == 2:
             for part in parts:
                 beyond[:, part] = matmul(hartley[own_m(1 - side), :], lowered[:, part]).astype(jnp.bfloat16)
@@ -667,17 +671,26 @@
             total[:, here] = product if first else total[:, here] + product
         return use
 
+    def double(here, value):
+        total[:, here] += 2.0 * value * vertical[:, here]
+
     def last(here, value):
-        flux[:, here] = (total[:, here] + 2.0 * value * vertical[:, here]).astype(jnp.bfloat16)
+        flux[:, here] = (value * vertical[:, here]).astype(jnp.bfloat16)
+        summed[:, here] = (total[:, here] + value * other[:, here]).astype(jnp.bfloat16)
 
     table_copy.wait()
     gather(0, keep(vertical))
-    for h, f in ((1, 0), (3, 1), (5, 3)):
-        gather(h, keep(other))
-        gather(h + 1, multiply(h == 1))
-        finish(f)
+    gather(1, keep(other))
+    gather(2, multiply(True))
+    finish(0)
+    gather(3, keep(other))
+    gather(4, multiply(False))
+    finish(1)
+    gather(5, keep(other))
+    gather(6, double)
     gather(7, last)
     finish(2)
+    finish(3)
 
     def settle(f):
         wait(landed.at[f], out_recv.at[f])
@@ -692,13 +705,13 @@
         def lay(step, carry):
             here = pl.ds(pl.multiple_of(step * chunk, chunk), chunk)
             stage[step, pl.ds(f, local_k, stride=fields), :] = wide[here, :].T
-            if f == 2:
+            if f == 3:
                 out[step] = stage[step].astype(jnp.bfloat16)
             return carry
 
-        lax.fori_loop(0, columns // chunk, lay, 0, unroll=f == 2)
-
-    for f in (0, 1, 3, 2):
+        lax.fori_loop(0, columns // chunk, lay, 0, unroll=f >= 2)
+
+    for f in (0, 1, 2, 3):
         settle(f)
 
     wait(rows.at[pl.ds(0, fields)], in_send)
@@ -741,6 +754,7 @@
             pltpu.VMEM((points_x, MZ), jnp.float32),
             pltpu.VMEM((points_x, MZ), jnp.float32),
             pltpu.VMEM((points_x, MZ), jnp.float32),
+            pltpu.VMEM((points_x, MZ), bf16),
             pltpu.VMEM((points_x, MZ), bf16),
             pltpu.VMEM((points_x, modes_z), bf16),
             pltpu.VMEM((fields, members * local_m, modes_z), bf16),

time: 104 us -> 103 us (level)
  no operation moved by 1% of the time
where the time goes in v6:
time: 103 us; the launch traced here: 102 us
  Pallas kernels  102 us (99%)
    pallas_call x1, Pallas kernels, on_device(): pl.pallas_call(functools.partial(body, nkx, ncz, pieces), out_shape=jax.S...  101 us

profile of v6, /device:TPU:0, one launch (start us, length us, event | category | flops | bytes accessed | tf_op | source)
XLA Modules:
  0.0 102.5 jit_solution(12793615567425498301)
XLA Ops:
  0.0 101.3 %shard_map.37 = bf16[12,512,128]{2,1,0:T(8,128)(2,1)S(1)} custom-call(bf16[128,4,1536]{2,1,0:T(4,128)(2,1)} %field_modes.1, bf16[128,4,1536]{2,1,0:T(4,128)(2,1)} %cotangent.1, bf16[1792,768]{1,0:T(8,128)(2,1)} %constant.2.clone.tables_in), custom_call_target="tpu_custom_call" | custom-call | tf_op jit(solution)/shard_map/pallas_call | solution.py:782
  101.3 1.1 %shard_map.38 = bf16[128,4,1536]{2,1,0:T(4,128)(2,1)} custom-call(bf16[12,128,4,128]{3,2,1,0:T(4,128)(2,1)S(1)} %bitcast.1), custom_call_target="tpu_custom_call" | custom-call | tf_op jit(solution)/shard_map/pallas_call | solution.py:799

commit v7 on v6

--- a/solution.py
+++ b/solution.py
@@ -536,7 +536,7 @@
         return target
 
     within = list(range(1, members))
-    across = [s for p in range(members // 2, places) for s in (2 * p + 1, 2 * p)]
+    across = [s for p in range(places - 1, members // 2 - 1, -1) for s in (2 * p + 1, 2 * p)]
 
     def to_all(steps, send):
         def one(step, carry):
@@ -601,7 +601,7 @@
     def launch(h):
         if h < 2 * fields:
             prepare(h)
-            to_all([0] + within + (across if shared[h] else []), functools.partial(send_in, h))
+            to_all((across if shared[h] else []) + [0] + within, functools.partial(send_in, h))
             keep_in(h)
 
     for h in range(1, ahead):
@@ -709,7 +709,7 @@
                 out[step] = stage[step].astype(jnp.bfloat16)
             return carry
 
-        lax.fori_loop(0, columns // chunk, lay, 0, unroll=f >= 2)
+        lax.fori_loop(0, columns // chunk, lay, 0, unroll=f == 3)
 
     for f in (0, 1, 2, 3):
         settle(f)

time: 103 us -> 103 us (level)
  no operation moved by 1% of the time
where the time goes in v7:
time: 103 us; the launch traced here: 102 us
  Pallas kernels  102 us (99%)
    pallas_call x1, Pallas kernels, on_device(): pl.pallas_call(functools.partial(body, nkx, ncz, pieces), out_shape=jax.S...  101 us

profile of v7, /device:TPU:0, one launch (start us, length us, event | category | flops | bytes accessed | tf_op | source)
XLA Modules:
  0.0 102.5 jit_solution(9050768979385223611)
XLA Ops:
  0.0 101.3 %shard_map.37 = bf16[12,512,128]{2,1,0:T(8,128)(2,1)S(1)} custom-call(bf16[128,4,1536]{2,1,0:T(4,128)(2,1)} %field_modes.1, bf16[128,4,1536]{2,1,0:T(4,128)(2,1)} %cotangent.1, bf16[1792,768]{1,0:T(8,128)(2,1)} %constant.2.clone.tables_in), custom_call_target="tpu_custom_call" | custom-call | tf_op jit(solution)/shard_map/pallas_call | solution.py:782
  101.3 1.1 %shard_map.38 = bf16[128,4,1536]{2,1,0:T(4,128)(2,1)} custom-call(bf16[12,128,4,128]{3,2,1,0:T(4,128)(2,1)S(1)} %bitcast.1), custom_call_target="tpu_custom_call" | custom-call | tf_op jit(solution)/shard_map/pallas_call | solution.py:799

commit v8 on v7

--- a/solution.py
+++ b/solution.py
@@ -435,7 +435,7 @@
     order = ((0, 2), (0, 0), (1, 0), (0, 1), (1, 1), (0, 3), (1, 2), (1, 3))
     shared = (True, False, True, False, True, False, False, True)
     place_of = [sum(shared[:h]) if shared[h] else h - sum(shared[:h]) for h in range(2 * fields)]
-    ahead = 6
+    ahead = 8
 
     places = nkx // 2
     place, column = i // 2, lax.rem(i, 2)

time: 103 us -> 103 us (level)
  no operation moved by 1% of the time
where the time goes in v8:
time: 103 us; the launch traced here: 102 us
  Pallas kernels  102 us (99%)
    pallas_call x1, Pallas kernels, on_device(): pl.pallas_call(functools.partial(body, nkx, ncz, pieces), out_shape=jax.S...  101 us

profile of v8, /device:TPU:0, one launch (start us, length us, event | category | flops | bytes accessed | tf_op | source)
XLA Modules:
  0.0 102.5 jit_solution(11563814913241984999)
XLA Ops:
  0.0 101.3 %shard_map.37 = bf16[12,512,128]{2,1,0:T(8,128)(2,1)S(1)} custom-call(bf16[128,4,1536]{2,1,0:T(4,128)(2,1)} %field_modes.1, bf16[128,4,1536]{2,1,0:T(4,128)(2,1)} %cotangent.1, bf16[1792,768]{1,0:T(8,128)(2,1)} %constant.2.clone.tables_in), custom_call_target="tpu_custom_call" | custom-call | tf_op jit(solution)/shard_map/pallas_call | solution.py:782
  101.3 1.1 %shard_map.38 = bf16[128,4,1536]{2,1,0:T(4,128)(2,1)} custom-call(bf16[12,128,4,128]{3,2,1,0:T(4,128)(2,1)S(1)} %bitcast.1), custom_call_target="tpu_custom_call" | custom-call | tf_op jit(solution)/shard_map/pallas_call | solution.py:799
